TPU v7x, 128 devices: a whole 4x4x4 slice. The times are simulated.
128 devices in a mesh: rec: 4 (over z), space: 32 (over y, x, core).
Axes of the slice: x: 4, y: 4, z: 4, core: 2. Of those that a mesh axis runs over, the one named last changes fastest.
Arguments:
- probes: bfloat16 [1048576, 128], P('space'), may hold values from -6 to 6
- band_coeffs: bfloat16 [16, 8, 1048576], P('rec', None, 'space'), may hold values from -2 to 2
- band_offsets: int32 [16, 8], P('rec'), may hold values from -128 to 128, as said below
Outputs:
- q_basis: float32 [1048576, 128], P(('space', 'rec'))
- r_factor: float32 [128, 128], replicated
Inputs may be any that keep to these rules, and one draw needn't show every extreme that they name: `band_offsets`: in every record band 0 has offset -128 and band 1 offset 128.
All inputs are finite; a program needn't handle non-finite values.
Results may differ from a plain program's by a relative error of at most 0.0003.
Values may be sent and summed in bfloat16 or wider, within the bound.
A program may use at most 128 MiB of HBM per device.

v0:
```python
import jax
import jax.numpy as jnp
from jax import lax
from jax.sharding import PartitionSpec as P

HALO = 128


def padded_2(cells, sides, width):
    for axis, dim in sides:
        count = lax.axis_size(axis)
        ends = count - 1
        head = lax.slice_in_dim(cells, 0, width, axis=dim)
        tail = lax.slice_in_dim(cells, cells.shape[dim] - width, cells.shape[dim], axis=dim)
        cells = jnp.concatenate(
            [
                lax.ppermute(tail, axis, [(i, (i + 1) % count) for i in range(ends)]),
                cells,
                lax.ppermute(head, axis, [((i + 1) % count, i) for i in range(ends)]),
            ],
            axis=dim,
        )
    return cells


def accumulate(padded, coeffs, offsets, row_start, count, margin):
    width = padded.shape[1]
    total = jnp.zeros((count, width), jnp.float32)
    for record in range(coeffs.shape[0]):
        for band in range(coeffs.shape[1]):
            offset = offsets[record, band]
            piece = lax.dynamic_slice_in_dim(padded, row_start + margin + offset, count, 0)
            coeff = coeffs[record, band]
            total = total + coeff.astype(jnp.float32)[:, None] * piece.astype(jnp.float32)
    return total


def local(probes, band_coeffs, band_offsets):
    rows = probes.shape[0]
    margin = HALO
    padded = padded_2(probes, (("space", 0),), margin)
    share = rows // lax.axis_size("rec")
    sketch = lax.psum_scatter(
        accumulate(
            padded, band_coeffs, band_offsets, jnp.int32(0), lax.axis_size("rec") * share, margin
        ),
        "rec",
        scatter_dimension=0,
        tiled=True,
    )
    local_gram = jnp.dot(
        sketch.T, sketch, precision=lax.Precision.HIGHEST, preferred_element_type=jnp.float32
    )
    gram = lax.psum(local_gram, ("rec", "space"))
    upper = jnp.linalg.cholesky(gram).T
    scale = jnp.sqrt(jnp.float32(rows * lax.axis_size("space")))
    solved = jax.scipy.linalg.solve_triangular(upper.T, sketch.T, lower=True)
    return (solved.T * scale, upper / scale)


def solution(mesh):
    in_specs = (P("space", None), P("rec", None, "space"), P("rec", None))
    out_specs = (P(("space", "rec"), None), P())
    return jax.shard_map(local, mesh=mesh, in_specs=in_specs, out_specs=out_specs, check_vma=False)
```

profile of v0, /device:TPU:1, one launch (start us, length us, event | category | flops | bytes accessed | tf_op | source)
XLA Modules:
  0.0 890.1 jit_solution(6260652256925387998)
XLA Ops:
  7.2 0.0 reduce-scatter.2.cloned.1.call-start
  7.2 1.4 fusion.2
  8.6 3.3 collective-permute-start.1
  11.9 3.1 collective-permute-start
  15.0 5.8 slice_convert_fusion.30
  20.8 6.8 slice_convert_fusion.31
  27.6 2.1 fusion.3
  29.7 1.9 fusion.4
  71.7 0.0 copy-start
  71.7 0.0 copy-start.1
  71.7 0.0 copy-start.2
  71.7 0.0 copy-start.3
  71.7 0.0 copy-start.4
  71.7 0.0 collective-permute-done
  71.7 0.8 constant_dynamic-update-slice_fusion.2
  72.6 4.5 constant_dynamic-update-slice_fusion.1
  77.1 0.0 collective-permute-done.1
  77.1 0.8 constant_dynamic-update-slice_fusion
  77.9 0.0 copy-done
  77.9 0.0 copy-done.1
  77.9 0.0 copy-done.2
  77.9 0.0 copy-done.3
  77.9 0.0 copy-done.4
  77.9 472.8 %multiply_add_fusion = f32[32768,128]{1,0:T(8,128)} fusion(bf16[33024,128]{1,0:T(8,128)(2,1)S(1)} %constant_dynamic-update-slice_fusion, s32[]{:T(128)S(6)} %select_n.131, f32[32768]{0:T(1024)S(1)} %bitcast.140, s32[]{:T(128)S(6)} %select_n.130, f32[32768]{0:T(1024)S(1)} %bitcast.141, s32[]{:T(128)S(6)} %select_n.129, f32[32768]{0:T(1024)S(1)} %bitcast.111, ...), kind=kLoop, calls=%fused_computation | loop fusion | flops 398458880 | bytes 289407104 | tf_op jit(solution)/shard_map/add | solution.py:34
  550.7 0.0 reduce-scatter.2.cloned.1.call-update
  550.7 0.2 all-reduce.2.cloned.1.call-start
  551.0 151.9 %reduce-scatter.2.cloned.1.call-done = f32[8192,128]{1,0:T(8,128)} async-done(((f32[32768,128]{1,0:T(8,128)}), f32[8192,128]{1,0:T(8,128)}) %reduce-scatter.2.cloned.1.call-update) | async-done | bytes 4194320 | tf_op jit(solution)/shard_map/reduce_scatter | solution.py:43
  702.9 10.8 %fusion.5 = f32[128,128]{0,1:T(8,128)} fusion(f32[8192,128]{1,0:T(8,128)} %reduce-scatter.2.cloned.1.call-done), kind=kOutput, calls=%fused_computation.50 | convolution fusion | flops 1610612736 | bytes 4259840 | tf_op jit(solution)/shard_map/dot_general | solution.py:51
  713.7 0.0 all-reduce.2.cloned.1.call-update
  713.8 137.5 %all-reduce.2.cloned.1.call-done = f32[128,128]{0,1:T(8,128)} async-done(((f32[128,128]{0,1:T(8,128)}), f32[128,128]{0,1:T(8,128)}) %all-reduce.2.cloned.1.call-update) | async-done | bytes 65552 | tf_op jit(solution)/shard_map/psum | solution.py:54
  851.2 0.9 copy.6
  852.2 0.9 fusion.1
  853.0 11.7 %cholesky.16 = f32[128,128]{1,0:T(8,128)S(1)} custom-call(f32[128,128]{1,0:T(8,128)S(1)} %fusion.1), custom_call_target="Cholesky" | custom-call | tf_op jit(solution)/shard_map/jit(cholesky)/cholesky | solution.py:55
  864.8 0.6 compare_reduce_fusion
  865.4 0.7 multiply_bitcast_fusion
  866.1 0.7 copy.7
  866.8 10.0 %custom-call.7 = f32[1,128,128]{1,2,0:T(8,128)S(1)} custom-call(f32[1,128,128]{2,1,0:T(8,128)S(1)} %get-tuple-element.39), custom_call_target="InvertDiagBlocksLowerTriangular" | custom-call | tf_op jit(solution)/shard_map/jit(_solve_triangular)/triangular_solve | solution.py:57
  876.8 6.5 convolution_multiply_fusion
  (1 shorter events, 0.0 us)
Async XLA Ops:
  7.2 695.7 %reduce-scatter.2.cloned.1.call-start = ((), (), s32[]{:S(2)}) async-start(), calls=%async_computation.1 | async-start | bytes 20971520 | tf_op jit(solution)/shard_map/reduce_scatter | solution.py:43
  8.6 68.5 %collective-permute-start.1 = (bf16[128,128]{1,0:T(8,128)(2,1)}, bf16[128,128]{1,0:T(8,128)(2,1)}, u32[]{:S(2)}, u32[]{:S(2)}) collective-permute-start(bf16[128,128]{1,0:T(8,128)(2,1)} %get-tuple-element.4), channel_id=1, source_target_pairs={{1,0},{2,1},{3,2},{4,3},{5,4},{6,5},{7,6},{8,7},{9,8},{10,9},{11,1... | collective-permute-start | bytes 98312 | tf_op jit(solution)/shard_map/ppermute | solution.py:19
  11.9 59.8 %collective-permute-start = (bf16[128,128]{1,0:T(8,128)(2,1)}, bf16[128,128]{1,0:T(8,128)(2,1)}, u32[]{:S(2)}, u32[]{:S(2)}) collective-permute-start(bf16[128,128]{1,0:T(8,128)(2,1)} %get-tuple-element.5), channel_id=1, source_target_pairs={{0,1},{1,2},{2,3},{3,4},{4,5},{5,6},{6,7},{7,8},{8,9},{9,10},{10,1... | collective-permute-start | bytes 98312 | tf_op jit(solution)/shard_map/ppermute | solution.py:17
  71.7 6.2 copy-start
  71.7 6.2 copy-start.1
  71.7 6.2 copy-start.2
  71.7 6.2 copy-start.3
  71.7 6.2 copy-start.4
  550.7 300.5 %all-reduce.2.cloned.1.call-start = ((), (), s32[]{:S(2)}) async-start(), calls=%async_computation.2 | async-start | bytes 131072 | tf_op jit(solution)/shard_map/psum | solution.py:54
Sparse Core Ops, SparseCore 0:
  550.9 151.9 reduce-scatter.1
  713.9 137.2 all-reduce.1
where the time goes:
time: 891 us; the launch traced here: 890 us
  other arithmetic  509 us (57%)
  waiting for transfers between devices  289 us (32%)
  between operations  54.3 us (6%)
  matrix products  17.3 us (2%)
  local copies, waits for them, and re-layouts  13.1 us (1%)
    add x1, other arithmetic, accumulate(): total + coeff.astype(jnp.float32)[:, None] * piece.astype(jnp.float32)  473 us
    reduce_scatter x1, waiting for transfers between devices, local(): lax.psum_scatter(accumulate(padded, band_coeffs, band_offsets, jnp.int32(...  152 us
    psum x1, waiting for transfers between devices, local(): gram = lax.psum(local_gram, ('rec', 'space'))  137 us
  transfers between devices with their start and end apart: 4, of which 2 were waited for; matrix products, arithmetic and copies ran while one was open for 2% of the time, Pallas kernels for 0%

commit v1 on v0

v1 whole, which is shorter than its diff:
```python
import functools
import math

import jax
import jax.numpy as jnp
from jax import lax
from jax.experimental import pallas as pl
from jax.experimental.pallas import tpu as pltpu
from jax.sharding import PartitionSpec as P

HALO = 128
B = 128
CHUNK = 1024
UNROLL = 4
MESH = pl.DeviceIdType.MESH
F32 = jnp.float32
BF16 = jnp.bfloat16


def dot(a, b, dims):
    return lax.dot_general(a, b, (dims, ((), ())), preferred_element_type=F32)


def split(x):
    high = x.astype(BF16)
    low = (x - high.astype(F32)).astype(BF16)
    return high, low


def sketch_kernel(
    nr, ns, c_hbm, o_hbm, p_hbm, hl_ref, g_ref,
    cbuf, obuf, sel, pbuf, c_send, c_recv, o_send, o_recv, h_send, h_recv, local_sem, own_sem,
):
    r = lax.axis_index("rec")
    s = lax.axis_index("space")
    share = cbuf.shape[1]
    nloc = c_hbm.shape[0]
    rows = p_hbm.shape[0]
    nch = share // CHUNK
    first, last = r == 0, r == nr - 1
    has_left, has_right = s > 0, s < ns - 1
    edge = jnp.logical_or(first, last)

    main = pltpu.make_async_copy(
        p_hbm.at[pl.ds(pl.multiple_of(r * share, share), share)],
        pbuf.at[pl.ds(HALO, share)], local_sem.at[0])
    main.start()

    def own_c(ch):
        return pltpu.make_async_copy(
            c_hbm.at[:, pl.ds(pl.multiple_of(r * share + ch * CHUNK, CHUNK), CHUNK)],
            cbuf.at[pl.ds(pl.multiple_of(r * nloc, nloc), nloc), pl.ds(pl.multiple_of(ch * CHUNK, CHUNK), CHUNK)],
            own_sem.at[ch])

    for ch in range(nch):
        own_c(ch).start()
    own_o = pltpu.make_async_copy(
        o_hbm, obuf.at[pl.ds(pl.multiple_of(r * nloc, nloc), nloc)], local_sem.at[1])
    own_o.start()

    barrier = pltpu.get_barrier_semaphore()
    for k in range(1, nr):
        pl.semaphore_signal(barrier, inc=1, device_id={"rec": lax.rem(r + k, nr)}, device_id_type=MESH)

    @pl.when(jnp.logical_and(edge, has_left))
    def _():
        pl.semaphore_signal(barrier, inc=1, device_id={"space": s - 1}, device_id_type=MESH)

    @pl.when(jnp.logical_and(edge, has_right))
    def _():
        pl.semaphore_signal(barrier, inc=1, device_id={"space": s + 1}, device_id_type=MESH)

    on_edge = edge.astype(jnp.int32)
    peers = nr - 1 + on_edge * (has_left.astype(jnp.int32) + has_right.astype(jnp.int32))
    pl.semaphore_wait(barrier, peers)

    def send_o(k):
        return pltpu.make_async_remote_copy(
            src_ref=o_hbm, dst_ref=obuf.at[pl.ds(pl.multiple_of(r * nloc, nloc), nloc)],
            send_sem=o_send.at[k - 1], recv_sem=o_recv.at[k - 1],
            device_id={"rec": lax.rem(r + k, nr)}, device_id_type=MESH)

    def recv_o(k):
        src = lax.rem(r + nr - k, nr)
        return pltpu.make_async_remote_copy(
            src_ref=o_hbm, dst_ref=obuf.at[pl.ds(pl.multiple_of(src * nloc, nloc), nloc)],
            send_sem=o_send.at[k - 1], recv_sem=o_recv.at[k - 1],
            device_id={"rec": lax.rem(r + k, nr)}, device_id_type=MESH)

    def send_c(k, ch):
        to = lax.rem(r + k, nr)
        return pltpu.make_async_remote_copy(
            src_ref=c_hbm.at[:, pl.ds(pl.multiple_of(to * share + ch * CHUNK, CHUNK), CHUNK)],
            dst_ref=cbuf.at[pl.ds(pl.multiple_of(r * nloc, nloc), nloc), pl.ds(pl.multiple_of(ch * CHUNK, CHUNK), CHUNK)],
            send_sem=c_send.at[k - 1, ch], recv_sem=c_recv.at[k - 1, ch],
            device_id={"rec": to}, device_id_type=MESH)

    def recv_c(k, ch):
        src = lax.rem(r + nr - k, nr)
        return pltpu.make_async_remote_copy(
            src_ref=c_hbm.at[:, pl.ds(0, CHUNK)],
            dst_ref=cbuf.at[pl.ds(pl.multiple_of(src * nloc, nloc), nloc), pl.ds(pl.multiple_of(ch * CHUNK, CHUNK), CHUNK)],
            send_sem=c_send.at[k - 1, ch], recv_sem=c_recv.at[k - 1, ch],
            device_id={"rec": lax.rem(r + k, nr)}, device_id_type=MESH)

    for k in range(1, nr):
        send_o(k).start()

    tail = pltpu.make_async_remote_copy(
        src_ref=p_hbm.at[pl.ds(rows - HALO, HALO)], dst_ref=pbuf.at[pl.ds(0, HALO)],
        send_sem=h_send.at[0], recv_sem=h_recv.at[0],
        device_id={"space": lax.rem(s + 1, ns)}, device_id_type=MESH)
    head = pltpu.make_async_remote_copy(
        src_ref=p_hbm.at[pl.ds(0, HALO)], dst_ref=pbuf.at[pl.ds(share + HALO, HALO)],
        send_sem=h_send.at[1], recv_sem=h_recv.at[1],
        device_id={"space": lax.rem(s + ns - 1, ns)}, device_id_type=MESH)

    @pl.when(jnp.logical_and(first, has_right))
    def _():
        tail.start()

    @pl.when(jnp.logical_and(last, has_left))
    def _():
        head.start()

    for ch in range(nch):
        for k in (2, 1, 3):
            send_c(k, ch).start()

    @pl.when(jnp.logical_and(first, s == 0))
    def _():
        pbuf[pl.ds(0, HALO), :] = jnp.zeros((HALO, pbuf.shape[1]), BF16)

    @pl.when(jnp.logical_and(last, s == ns - 1))
    def _():
        pbuf[pl.ds(share + HALO, HALO), :] = jnp.zeros((HALO, pbuf.shape[1]), BF16)

    @pl.when(r > 0)
    def _():
        cp = pltpu.make_async_copy(
            p_hbm.at[pl.ds(pl.multiple_of(r * share - HALO, HALO), HALO)],
            pbuf.at[pl.ds(0, HALO)], local_sem.at[2])
        cp.start()
        cp.wait()

    @pl.when(r < nr - 1)
    def _():
        cp = pltpu.make_async_copy(
            p_hbm.at[pl.ds(pl.multiple_of((r + 1) * share, HALO), HALO)],
            pbuf.at[pl.ds(share + HALO, HALO)], local_sem.at[3])
        cp.start()
        cp.wait()

    @pl.when(jnp.logical_and(first, has_left))
    def _():
        tail.wait_recv()

    @pl.when(jnp.logical_and(last, has_right))
    def _():
        head.wait_recv()

    own_o.wait()
    for k in range(1, nr):
        recv_o(k).wait_recv()
    off = obuf[...]
    lane = lax.broadcasted_iota(jnp.int32, (B, B), 1)
    for t in range(3):
        sel[:, t * B:(t + 1) * B] = jnp.where(lane + (t * B - HALO) == off, 1.0, 0.0).astype(BF16)
    main.wait()
    g_ref[...] = jnp.zeros_like(g_ref)

    def block(p0):
        cols = cbuf[:, pl.ds(p0, B)]
        diag = dot(cols, sel[...], ((0,), (0,)))
        band = pltpu.roll(diag, 0, 1, stride=1, stride_axis=0)
        bh, bl = split(band)
        piece = pbuf[pl.ds(p0, 3 * B), :]
        sk = dot(bh, piece, ((1,), (0,))) + dot(bl, piece, ((1,), (0,)))
        hi, lo = split(sk)
        hl_ref[pl.ds(p0, B), 0:B] = hi
        hl_ref[pl.ds(p0, B), B:2 * B] = lo

    def step(i, _):
        base = pl.multiple_of(i * (UNROLL * B), UNROLL * B)
        for u in range(UNROLL):
            block(base + u * B)
        hl = hl_ref[pl.ds(base, UNROLL * B), :]
        g_ref[...] += dot(hl, hl, ((0,), (0,)))
        return 0

    def chunk(ch, _):
        own_c(ch).wait()
        for k in (1, 3, 2):
            recv_c(k, ch).wait_recv()
        per = CHUNK // (UNROLL * B)
        lax.fori_loop(ch * per, (ch + 1) * per, step, 0)
        return 0

    lax.fori_loop(0, nch, chunk, 0)

    for k in range(1, nr):
        send_o(k).wait_send()
        for ch in range(nch):
            send_c(k, ch).wait_send()

    @pl.when(jnp.logical_and(first, has_right))
    def _():
        tail.wait_send()

    @pl.when(jnp.logical_and(last, has_left))
    def _():
        head.wait_send()


def factor_kernel(scale, hl_ref, g_ref, q_ref, u_ref, w_ref):
    n = g_ref.shape[0]

    @pl.when(pl.program_id(0) == 0)
    def _():
        a = g_ref[...]
        rowi = lax.broadcasted_iota(jnp.int32, (n, n), 0)
        lane = lax.broadcasted_iota(jnp.int32, (n, n), 1)
        eye = jnp.where(rowi == lane, 1.0, 0.0).astype(F32)
        nt = n // 8
        at = [a[8 * t:8 * t + 8] for t in range(nt)]
        it = [eye[8 * t:8 * t + 8] for t in range(nt)]
        sub = lax.broadcasted_iota(jnp.int32, (8, n), 0)
        for j in range(n):
            t0 = j // 8
            ra = jnp.broadcast_to(at[t0][j % 8:j % 8 + 1, :], (8, n))
            ri = jnp.broadcast_to(it[t0][j % 8:j % 8 + 1, :], (8, n))
            piv = jnp.broadcast_to(ra[:, j:j + 1], (8, n))
            inv = 1.0 / piv
            ra = ra * inv
            ri = ri * inv
            for t in range(t0, nt):
                if t == t0 and j % 8 == 7:
                    continue
                col = jnp.broadcast_to(at[t][:, j:j + 1], (8, n))
                if t == t0:
                    col = jnp.where(sub > j % 8, col, 0.0)
                at[t] = at[t] - col * ra
                it[t] = it[t] - col * ri
        a = jnp.concatenate(at, axis=0)
        linv = jnp.concatenate(it, axis=0)
        diag = jnp.sum(jnp.where(rowi == lane, a, 0.0), axis=1, keepdims=True)
        rs = 1.0 / jnp.sqrt(diag)
        u_ref[...] = jnp.where(lane >= rowi, a, 0.0) * (rs * (1.0 / scale))
        linv = jnp.where(lane <= rowi, linv, 0.0) * (rs * scale)
        right = linv.T
        rh, rl = split(right)
        w_ref[0:n, 0:n] = rh
        w_ref[0:n, n:2 * n] = rl
        w_ref[n:2 * n, 0:n] = rh
        w_ref[n:2 * n, n:2 * n] = jnp.zeros((n, n), BF16)

    out = dot(hl_ref[...], w_ref[...], ((1,), (0,)))
    q_ref[...] = out[:, :n] + out[:, n:]


def local(nr, ns, probes, band_coeffs, band_offsets):
    rows, k = probes.shape
    share = rows // nr
    nloc = band_coeffs.shape[0] * band_coeffs.shape[1]
    nall = nr * nloc
    nch = share // CHUNK
    coeffs = band_coeffs.reshape(nloc, rows)
    offs = jnp.broadcast_to(band_offsets.reshape(nloc, 1), (nloc, B))
    any_spec = pl.BlockSpec(memory_space=pl.ANY)
    vmem_spec = pl.BlockSpec(memory_space=pltpu.VMEM)
    dma = pltpu.SemaphoreType.DMA
    hl, g = pl.pallas_call(
        functools.partial(sketch_kernel, nr, ns),
        out_shape=(jax.ShapeDtypeStruct((share, 2 * k), BF16), jax.ShapeDtypeStruct((2 * k, 2 * k), F32)),
        in_specs=[any_spec] * 3,
        out_specs=(vmem_spec, vmem_spec),
        scratch_shapes=[
            pltpu.VMEM((nall, share), BF16),
            pltpu.VMEM((nall, B), jnp.int32),
            pltpu.VMEM((nall, 3 * B), BF16),
            pltpu.VMEM((share + 2 * HALO, k), BF16),
            dma((nr - 1, nch)), dma((nr - 1, nch)),
            dma((nr - 1,)), dma((nr - 1,)), dma((2,)), dma((2,)), dma((4,)), dma((nch,)),
        ],
        compiler_params=pltpu.CompilerParams(
            collective_id=0, has_side_effects=True, vmem_limit_bytes=48 << 20),
    )(coeffs, offs, probes)
    gram = g[:k, :k] + g[:k, k:] + g[k:, :k] + g[k:, k:]
    gram = lax.psum(gram, ("rec", "space"))
    scale = math.sqrt(rows * ns)
    tile = 1024
    q, u = pl.pallas_call(
        functools.partial(factor_kernel, scale),
        grid=(share // tile,),
        out_shape=(jax.ShapeDtypeStruct((share, k), F32), jax.ShapeDtypeStruct((k, k), F32)),
        in_specs=[pl.BlockSpec((tile, 2 * k), lambda i: (i, 0)), pl.BlockSpec((k, k), lambda i: (0, 0))],
        out_specs=(pl.BlockSpec((tile, k), lambda i: (i, 0)), pl.BlockSpec((k, k), lambda i: (0, 0))),
        scratch_shapes=[pltpu.VMEM((2 * k, 2 * k), BF16)],
        compiler_params=pltpu.CompilerParams(dimension_semantics=("arbitrary",)),
    )(hl, gram)
    return q, u


def solution(mesh):
    in_specs = (P("space", None), P("rec", None, "space"), P("rec", None))
    out_specs = (P(("space", "rec"), None), P())
    body = functools.partial(local, mesh.shape["rec"], mesh.shape["space"])
    return jax.shard_map(body, mesh=mesh, in_specs=in_specs, out_specs=out_specs, check_vma=False)
```

time: 891 us -> 220 us (0.25)
  other arithmetic: 509 us -> 0.64 us
  waiting for transfers between devices: 289 us -> 138 us
  Pallas kernels: 0 us -> 64.2 us
  between operations: 54.3 us -> 14 us
  matrix products: 17.3 us -> 0 us
  local copies, waits for them, and re-layouts: 13.1 us -> 2.43 us
    add x1, other arithmetic: 473 us -> 0.64 us  [local(): gram = g[:k, :k] + g[:k, k:] + g[k:, :k] + g[k:, k:]]
    reduce_scatter x1 -> x0, waiting for transfers between devices: 152 us -> none  [local(): lax.psum_scatter(accumulate(padded, band_coeffs, band_offsets, jnp.int32(...]
    pallas_call x0 -> x2, Pallas kernels: none -> 64.2 us  [the longest x1 39.5 us: local(): pl.pallas_call(functools.partial(sketch_kernel, nr, ns), out_shape=(jax.S...]
    another operation x4 -> x0, other arithmetic: 22.4 us -> none  [the longest x3 12.4 us: local(): upper = jnp.linalg.cholesky(gram).T]
    convert_element_type x2 -> x0, other arithmetic: 12.6 us -> none  [accumulate(): coeff.astype(jnp.float32)[:, None] * piece.astype(jnp.float32)]
    dot_general x1 -> x0, matrix products: 10.8 us -> none  [local(): jnp.dot(sketch.T, sketch, precision=lax.Precision.HIGHEST, preferred_elem...]
  transfers between devices with their start and end apart: 4 -> 1, of which waited for: 2 -> 1; matrix products, arithmetic and copies ran while one was open for 2% -> 0% of each run, Pallas kernels for 0% -> 0%
where the time goes in v1:
time: 220 us; the launch traced here: 219 us
  waiting for transfers between devices  138 us (63%)
  Pallas kernels  64.2 us (29%)
  between operations  14 us (6%)
  local copies, waits for them, and re-layouts  2.43 us (1%)
    psum x1, waiting for transfers between devices, local(): gram = lax.psum(gram, ('rec', 'space'))  138 us
    pallas_call x1, Pallas kernels, local(): pl.pallas_call(functools.partial(sketch_kernel, nr, ns), out_shape=(jax.S...  39.5 us
    pallas_call x1, Pallas kernels, local(): pl.pallas_call(functools.partial(factor_kernel, scale), grid=(share // ti...  24.7 us
  transfers between devices with their start and end apart: 1, of which 1 were waited for; matrix products, arithmetic and copies ran while one was open for 0% of the time, Pallas kernels for 0%

profile of v1, /device:TPU:1, one launch (start us, length us, event | category | flops | bytes accessed | tf_op | source)
XLA Modules:
  0.0 219.5 jit_solution(12985979310554118433)
XLA Ops:
  7.2 0.0 all-reduce.2.cloned.1.call-start
  7.2 0.8 broadcast_in_dim.7
  8.0 0.1 broadcast_in_dim.8.o_hbm
  8.0 0.0 copy-start
  8.0 1.6 copy-done
  9.6 39.5 %shard_map.50 = (bf16[8192,256]{1,0:T(8,128)(2,1)}, f32[256,256]{1,0:T(8,128)S(1)}) custom-call(bf16[32,32768]{1,0:T(8,128)(2,1)S(1)} %bitcast.1, s32[32,128]{1,0:T(8,128)S(1)} %broadcast_in_dim.8.o_hbm, bf16[32768,128]{1,0:T(8,128)(2,1)} %p_hbm.1), custom_call_target="tpu_custom_call" | custom-call | tf_op jit(solution)/shard_map/pallas_call | solution.py:272
  49.2 0.6 slice_add_fusion
  49.8 0.0 all-reduce.2.cloned.1.call-update
  49.8 138.1 %all-reduce.2.cloned.1.call-done.g_ref = f32[128,128]{1,0:T(8,128)} async-done(((f32[128,128]{1,0:T(8,128)}), f32[128,128]{1,0:T(8,128)}) %all-reduce.2.cloned.1.call-update) | async-done | bytes 65552 | tf_op jit(solution)/shard_map/psum | solution.py:289
  188.0 24.7 %shard_map.51 = (f32[8192,128]{1,0:T(8,128)}, f32[128,128]{1,0:T(8,128)}) custom-call(bf16[8192,256]{1,0:T(8,128)(2,1)} %get-tuple-element.4.hl_ref, f32[128,128]{1,0:T(8,128)} %all-reduce.2.cloned.1.call-done.g_ref), custom_call_target="tpu_custom_call" | custom-call | tf_op jit(solution)/shard_map/pallas_call | solution.py:292
Async XLA Ops:
  7.2 180.8 %all-reduce.2.cloned.1.call-start = ((), (), s32[]{:S(2)}) async-start(), calls=%async_computation | async-start | bytes 131072 | tf_op jit(solution)/shard_map/psum | solution.py:289
  8.0 1.6 copy-start
Sparse Core Ops, SparseCore 0:
  50.0 137.9 all-reduce.1

commit v2 on v1

--- a/solution.py
+++ b/solution.py
@@ -9,6 +9,7 @@
 from jax.sharding import PartitionSpec as P
 
 HALO = 128
+SIDE = 4
 B = 128
 CHUNK = 1024
 UNROLL = 4
@@ -28,8 +29,10 @@
 
 
 def sketch_kernel(
-    nr, ns, c_hbm, o_hbm, p_hbm, hl_ref, g_ref,
-    cbuf, obuf, sel, pbuf, c_send, c_recv, o_send, o_recv, h_send, h_recv, local_sem, own_sem,
+    nr, ns, c_hbm, o_hbm, p_hbm, hl_ref, out_ref,
+    cbuf, obuf, sel, pbuf, g_ref, gsum, gpart, gx, gy, gall,
+    c_send, c_recv, o_send, o_recv, h_send, h_recv, local_sem, own_sem,
+    s_send, s_recv, x_send, x_recv, y_send, y_recv, a_send, a_recv,
 ):
     r = lax.axis_index("rec")
     s = lax.axis_index("space")
@@ -58,21 +61,37 @@
         o_hbm, obuf.at[pl.ds(pl.multiple_of(r * nloc, nloc), nloc)], local_sem.at[1])
     own_o.start()
 
+    core = lax.rem(s, 2)
+    xi = lax.rem(s // 2, SIDE)
+    yi = s // (2 * SIDE)
+    octet = 2 * nr
+    mine = 2 * r + core
+
+    def cube_peer(k):
+        at = lax.rem(mine + k, octet)
+        return at, {"rec": at // 2, "space": s - core + lax.rem(at, 2)}
+
+    def x_peer(k):
+        return {"space": s + 2 * (lax.rem(xi + k, SIDE) - xi)}
+
+    def y_peer(k):
+        return {"space": s + 2 * SIDE * (lax.rem(yi + k, SIDE) - yi)}
+
     barrier = pltpu.get_barrier_semaphore()
-    for k in range(1, nr):
-        pl.semaphore_signal(barrier, inc=1, device_id={"rec": lax.rem(r + k, nr)}, device_id_type=MESH)
-
-    @pl.when(jnp.logical_and(edge, has_left))
-    def _():
-        pl.semaphore_signal(barrier, inc=1, device_id={"space": s - 1}, device_id_type=MESH)
-
-    @pl.when(jnp.logical_and(edge, has_right))
-    def _():
-        pl.semaphore_signal(barrier, inc=1, device_id={"space": s + 1}, device_id_type=MESH)
-
-    on_edge = edge.astype(jnp.int32)
-    peers = nr - 1 + on_edge * (has_left.astype(jnp.int32) + has_right.astype(jnp.int32))
-    pl.semaphore_wait(barrier, peers)
+    for k in range(1, octet):
+        pl.semaphore_signal(barrier, inc=1, device_id=cube_peer(k)[1], device_id_type=MESH)
+    for k in range(1, SIDE):
+        pl.semaphore_signal(barrier, inc=1, device_id=x_peer(k), device_id_type=MESH)
+        pl.semaphore_signal(barrier, inc=1, device_id=y_peer(k), device_id_type=MESH)
+
+    other = s + 2 * core - 1
+    has_other = jnp.logical_and(edge, jnp.logical_and(other >= 0, other < ns))
+
+    @pl.when(has_other)
+    def _():
+        pl.semaphore_signal(barrier, inc=1, device_id={"space": other}, device_id_type=MESH)
+
+    pl.semaphore_wait(barrier, octet - 1 + 2 * (SIDE - 1) + has_other.astype(jnp.int32))
 
     def send_o(k):
         return pltpu.make_async_remote_copy(
@@ -197,6 +216,50 @@
         return 0
 
     lax.fori_loop(0, nch, chunk, 0)
+
+    n = out_ref.shape[0]
+    part = n // octet
+    gsum[...] = (g_ref[0:n, 0:n] + g_ref[n:2 * n, n:2 * n]) + (g_ref[0:n, n:2 * n] + g_ref[n:2 * n, 0:n])
+
+    def exchange(copies):
+        for cp in copies:
+            cp.start()
+        for cp in copies:
+            cp.wait_recv()
+
+    def total(ref):
+        acc = ref[0]
+        for i in range(1, ref.shape[0]):
+            acc = acc + ref[i]
+        return acc
+
+    scatter = []
+    for k in range(1, octet):
+        at, to = cube_peer(k)
+        scatter.append(pltpu.make_async_remote_copy(
+            src_ref=gsum.at[pl.ds(pl.multiple_of(at * part, part), part)], dst_ref=gpart.at[mine],
+            send_sem=s_send.at[k - 1], recv_sem=s_recv.at[k - 1], device_id=to, device_id_type=MESH))
+    gpart[mine] = gsum[pl.ds(pl.multiple_of(mine * part, part), part), :]
+    exchange(scatter)
+    gx[xi] = total(gpart)
+    along_x = [pltpu.make_async_remote_copy(
+        src_ref=gx.at[xi], dst_ref=gx.at[xi], send_sem=x_send.at[k - 1], recv_sem=x_recv.at[k - 1],
+        device_id=x_peer(k), device_id_type=MESH) for k in range(1, SIDE)]
+    exchange(along_x)
+    gy[yi] = total(gx)
+    along_y = [pltpu.make_async_remote_copy(
+        src_ref=gy.at[yi], dst_ref=gy.at[yi], send_sem=y_send.at[k - 1], recv_sem=y_recv.at[k - 1],
+        device_id=y_peer(k), device_id_type=MESH) for k in range(1, SIDE)]
+    exchange(along_y)
+    own = pl.ds(pl.multiple_of(mine * part, part), part)
+    gall[own, :] = total(gy)
+    gather = [pltpu.make_async_remote_copy(
+        src_ref=gall.at[own], dst_ref=gall.at[own], send_sem=a_send.at[k - 1], recv_sem=a_recv.at[k - 1],
+        device_id=cube_peer(k)[1], device_id_type=MESH) for k in range(1, octet)]
+    exchange(gather)
+    out_ref[...] = gall[...]
+    for cp in scatter + along_x + along_y + gather:
+        cp.wait_send()
 
     for k in range(1, nr):
         send_o(k).wait_send()
@@ -264,14 +327,15 @@
     nloc = band_coeffs.shape[0] * band_coeffs.shape[1]
     nall = nr * nloc
     nch = share // CHUNK
+    octet = 2 * nr
     coeffs = band_coeffs.reshape(nloc, rows)
     offs = jnp.broadcast_to(band_offsets.reshape(nloc, 1), (nloc, B))
     any_spec = pl.BlockSpec(memory_space=pl.ANY)
     vmem_spec = pl.BlockSpec(memory_space=pltpu.VMEM)
     dma = pltpu.SemaphoreType.DMA
-    hl, g = pl.pallas_call(
+    hl, gram = pl.pallas_call(
         functools.partial(sketch_kernel, nr, ns),
-        out_shape=(jax.ShapeDtypeStruct((share, 2 * k), BF16), jax.ShapeDtypeStruct((2 * k, 2 * k), F32)),
+        out_shape=(jax.ShapeDtypeStruct((share, 2 * k), BF16), jax.ShapeDtypeStruct((k, k), F32)),
         in_specs=[any_spec] * 3,
         out_specs=(vmem_spec, vmem_spec),
         scratch_shapes=[
@@ -279,14 +343,20 @@
             pltpu.VMEM((nall, B), jnp.int32),
             pltpu.VMEM((nall, 3 * B), BF16),
             pltpu.VMEM((share + 2 * HALO, k), BF16),
+            pltpu.VMEM((2 * k, 2 * k), F32),
+            pltpu.VMEM((k, k), F32),
+            pltpu.VMEM((octet, k // octet, k), F32),
+            pltpu.VMEM((SIDE, k // octet, k), F32),
+            pltpu.VMEM((SIDE, k // octet, k), F32),
+            pltpu.VMEM((k, k), F32),
             dma((nr - 1, nch)), dma((nr - 1, nch)),
             dma((nr - 1,)), dma((nr - 1,)), dma((2,)), dma((2,)), dma((4,)), dma((nch,)),
+            dma((octet - 1,)), dma((octet - 1,)), dma((SIDE - 1,)), dma((SIDE - 1,)),
+            dma((SIDE - 1,)), dma((SIDE - 1,)), dma((octet - 1,)), dma((octet - 1,)),
         ],
         compiler_params=pltpu.CompilerParams(
             collective_id=0, has_side_effects=True, vmem_limit_bytes=48 << 20),
     )(coeffs, offs, probes)
-    gram = g[:k, :k] + g[:k, k:] + g[k:, :k] + g[k:, k:]
-    gram = lax.psum(gram, ("rec", "space"))
     scale = math.sqrt(rows * ns)
     tile = 1024
     q, u = pl.pallas_call(

time: 220 us -> 86.6 us (0.39)
  waiting for transfers between devices: 138 us -> 0 us
  Pallas kernels: 64.2 us -> 82.5 us
  between operations: 14 us -> 0.65 us
    psum x1 -> x0, waiting for transfers between devices: 138 us -> none  [local(): gram = lax.psum(gram, ('rec', 'space'))]
    pallas_call x1, Pallas kernels: 39.5 us -> 57.9 us  [local(): pl.pallas_call(functools.partial(sketch_kernel, nr, ns), out_shape=(jax.S...]
  transfers between devices with their start and end apart: 1 -> 0, of which waited for: 1 -> 0; matrix products, arithmetic and copies ran while one was open for 0% -> 0% of each run, Pallas kernels for 0% -> 0%
where the time goes in v2:
time: 86.6 us; the launch traced here: 86.2 us
  Pallas kernels  82.5 us (95%)
  local copies, waits for them, and re-layouts  3.04 us (4%)
    pallas_call x1, Pallas kernels, local(): pl.pallas_call(functools.partial(sketch_kernel, nr, ns), out_shape=(jax.S...  57.9 us
    pallas_call x1, Pallas kernels, local(): pl.pallas_call(functools.partial(factor_kernel, scale), grid=(share // ti...  24.7 us
    unnamed x4, local copies, waits for them, and re-layouts  2.2 us

profile of v2, /device:TPU:1, one launch (start us, length us, event | category | flops | bytes accessed | tf_op | source)
XLA Modules:
  0.0 86.2 jit_solution(1993523777577553689)
XLA Ops:
  0.6 0.8 broadcast_in_dim.7
  1.4 0.1 broadcast_in_dim.8.o_hbm
  1.5 0.0 copy-start
  1.5 1.6 %copy-done = bf16[4,8,32768]{2,1,0:T(8,128)(2,1)S(1)} copy-done((bf16[4,8,32768]{2,1,0:T(8,128)(2,1)S(1)}, bf16[4,8,32768]{2,1,0:T(8,128)(2,1)}, u32[]{:S(2)}) %copy-start) | copy-done | bytes 2097176
  3.1 57.9 %shard_map.50 = (bf16[8192,256]{1,0:T(8,128)(2,1)}, f32[128,128]{1,0:T(8,128)S(1)}) custom-call(bf16[32,32768]{1,0:T(8,128)(2,1)S(1)} %bitcast.1, s32[32,128]{1,0:T(8,128)S(1)} %broadcast_in_dim.8.o_hbm, bf16[32768,128]{1,0:T(8,128)(2,1)} %p_hbm.1), custom_call_target="tpu_custom_call" | custom-call | tf_op jit(solution)/shard_map/pallas_call | solution.py:336
  60.9 0.0 copy-start.1
  60.9 0.6 copy-done.1
  61.5 24.7 %shard_map.51 = (f32[8192,128]{1,0:T(8,128)}, f32[128,128]{1,0:T(8,128)}) custom-call(bf16[8192,256]{1,0:T(8,128)(2,1)} %get-tuple-element.4.hl_ref, f32[128,128]{1,0:T(8,128)} %copy-done.1), custom_call_target="tpu_custom_call" | custom-call | tf_op jit(solution)/shard_map/pallas_call | solution.py:362
Async XLA Ops:
  1.5 1.6 %copy-start = (bf16[4,8,32768]{2,1,0:T(8,128)(2,1)S(1)}, bf16[4,8,32768]{2,1,0:T(8,128)(2,1)}, u32[]{:S(2)}) copy-start(bf16[4,8,32768]{2,1,0:T(8,128)(2,1)} %param.4) | copy-start | bytes 6291460
  60.9 0.6 copy-start.1

commit v3 on v2

--- a/solution.py
+++ b/solution.py
@@ -29,9 +29,9 @@
 
 
 def sketch_kernel(
-    nr, ns, c_hbm, o_hbm, p_hbm, hl_ref, out_ref,
-    cbuf, obuf, sel, pbuf, g_ref, gsum, gpart, gx, gy, gall,
-    c_send, c_recv, o_send, o_recv, h_send, h_recv, local_sem, own_sem,
+    nr, ns, c_hbm, o_hbm, p_hbm, hl_hbm, out_ref,
+    hl_ref, cbuf, obuf, sel, pbuf, g_ref, gsum, gpart, gx, gy, gall,
+    c_send, c_recv, o_send, o_recv, h_send, h_recv, local_sem, own_sem, out_sem,
     s_send, s_recv, x_send, x_recv, y_send, y_recv, a_send, a_recv,
 ):
     r = lax.axis_index("rec")
@@ -207,12 +207,17 @@
         g_ref[...] += dot(hl, hl, ((0,), (0,)))
         return 0
 
+    def store_hl(ch):
+        here = pl.ds(pl.multiple_of(ch * CHUNK, CHUNK), CHUNK)
+        return pltpu.make_async_copy(hl_ref.at[here], hl_hbm.at[here], out_sem.at[ch])
+
     def chunk(ch, _):
         own_c(ch).wait()
         for k in (1, 3, 2):
             recv_c(k, ch).wait_recv()
         per = CHUNK // (UNROLL * B)
         lax.fori_loop(ch * per, (ch + 1) * per, step, 0)
+        store_hl(ch).start()
         return 0
 
     lax.fori_loop(0, nch, chunk, 0)
@@ -258,6 +263,8 @@
         device_id=cube_peer(k)[1], device_id_type=MESH) for k in range(1, octet)]
     exchange(gather)
     out_ref[...] = gall[...]
+    for ch in range(nch):
+        store_hl(ch).wait()
     for cp in scatter + along_x + along_y + gather:
         cp.wait_send()
 
@@ -275,37 +282,63 @@
         head.wait_send()
 
 
-def factor_kernel(scale, hl_ref, g_ref, q_ref, u_ref, w_ref):
+def eliminate(a, eye, n):
+    nt = n // 8
+    at = [a[8 * t:8 * t + 8] for t in range(nt)]
+    it = [eye[8 * t:8 * t + 8] for t in range(nt)]
+    sub = lax.broadcasted_iota(jnp.int32, (8, n), 0)
+
+    def row(x, i):
+        return jnp.broadcast_to(x[i:i + 1, :], (8, n))
+
+    def col(x, j):
+        return jnp.broadcast_to(x[:, j:j + 1], (8, n))
+
+    for t0 in range(nt):
+        j = 8 * t0
+        head = [col(at[t0], j + i) for i in range(8)]
+        piv = [[row(head[i], k) if k >= i else None for k in range(8)] for i in range(8)]
+        inv, mult = [], [[None] * 8 for _ in range(8)]
+        for i in range(8):
+            inv.append(1.0 / piv[i][i])
+            for k in range(i + 1, 8):
+                mult[k][i] = piv[i][k] * inv[i]
+            for k in range(i + 1, 8):
+                for m in range(k, 8):
+                    piv[k][m] = piv[k][m] - mult[k][i] * piv[i][m]
+        ra = [row(at[t0], i) for i in range(8)]
+        ri = [row(it[t0], i) for i in range(8)]
+        for i in range(8):
+            for k in range(i + 1, 8):
+                ra[k] = ra[k] - mult[k][i] * ra[i]
+                ri[k] = ri[k] - mult[k][i] * ri[i]
+        sa = [x * v for x, v in zip(ra, inv)]
+        si = [x * v for x, v in zip(ri, inv)]
+        for t in range(t0, nt):
+            c = head if t == t0 else [col(at[t], j + i) for i in range(8)]
+            c = list(c)
+            for i in range(8):
+                for k in range(i + 1, 8):
+                    c[k] = c[k] - mult[k][i] * c[i]
+            for i in range(8):
+                f = jnp.where(sub > i, c[i], 0.0) if t == t0 else c[i]
+                at[t] = at[t] - f * sa[i]
+                it[t] = it[t] - f * si[i]
+    return jnp.concatenate(at, axis=0), jnp.concatenate(it, axis=0)
+
+
+def factor_kernel(scale, hl_hbm, g_ref, q_ref, u_ref, w_ref, hl_ref, sem):
     n = g_ref.shape[0]
+    tile = q_ref.shape[0]
 
     @pl.when(pl.program_id(0) == 0)
     def _():
-        a = g_ref[...]
+        fetch = pltpu.make_async_copy(hl_hbm, hl_ref, sem)
+        fetch.start()
         rowi = lax.broadcasted_iota(jnp.int32, (n, n), 0)
         lane = lax.broadcasted_iota(jnp.int32, (n, n), 1)
         eye = jnp.where(rowi == lane, 1.0, 0.0).astype(F32)
-        nt = n // 8
-        at = [a[8 * t:8 * t + 8] for t in range(nt)]
-        it = [eye[8 * t:8 * t + 8] for t in range(nt)]
-        sub = lax.broadcasted_iota(jnp.int32, (8, n), 0)
-        for j in range(n):
-            t0 = j // 8
-            ra = jnp.broadcast_to(at[t0][j % 8:j % 8 + 1, :], (8, n))
-            ri = jnp.broadcast_to(it[t0][j % 8:j % 8 + 1, :], (8, n))
-            piv = jnp.broadcast_to(ra[:, j:j + 1], (8, n))
-            inv = 1.0 / piv
-            ra = ra * inv
-            ri = ri * inv
-            for t in range(t0, nt):
-                if t == t0 and j % 8 == 7:
-                    continue
-                col = jnp.broadcast_to(at[t][:, j:j + 1], (8, n))
-                if t == t0:
-                    col = jnp.where(sub > j % 8, col, 0.0)
-                at[t] = at[t] - col * ra
-                it[t] = it[t] - col * ri
-        a = jnp.concatenate(at, axis=0)
-        linv = jnp.concatenate(it, axis=0)
+        a, linv = eliminate(g_ref[...], eye, n)
         diag = jnp.sum(jnp.where(rowi == lane, a, 0.0), axis=1, keepdims=True)
         rs = 1.0 / jnp.sqrt(diag)
         u_ref[...] = jnp.where(lane >= rowi, a, 0.0) * (rs * (1.0 / scale))
@@ -316,8 +349,10 @@
         w_ref[0:n, n:2 * n] = rl
         w_ref[n:2 * n, 0:n] = rh
         w_ref[n:2 * n, n:2 * n] = jnp.zeros((n, n), BF16)
-
-    out = dot(hl_ref[...], w_ref[...], ((1,), (0,)))
+        fetch.wait()
+
+    here = pl.ds(pl.multiple_of(pl.program_id(0) * tile, tile), tile)
+    out = dot(hl_ref[here, :], w_ref[...], ((1,), (0,)))
     q_ref[...] = out[:, :n] + out[:, n:]
 
 
@@ -330,15 +365,16 @@
     octet = 2 * nr
     coeffs = band_coeffs.reshape(nloc, rows)
     offs = jnp.broadcast_to(band_offsets.reshape(nloc, 1), (nloc, B))
-    any_spec = pl.BlockSpec(memory_space=pl.ANY)
+    hbm_spec = pl.BlockSpec(memory_space=pltpu.HBM)
     vmem_spec = pl.BlockSpec(memory_space=pltpu.VMEM)
     dma = pltpu.SemaphoreType.DMA
     hl, gram = pl.pallas_call(
         functools.partial(sketch_kernel, nr, ns),
         out_shape=(jax.ShapeDtypeStruct((share, 2 * k), BF16), jax.ShapeDtypeStruct((k, k), F32)),
-        in_specs=[any_spec] * 3,
-        out_specs=(vmem_spec, vmem_spec),
+        in_specs=[hbm_spec] * 3,
+        out_specs=(hbm_spec, vmem_spec),
         scratch_shapes=[
+            pltpu.VMEM((share, 2 * k), BF16),
             pltpu.VMEM((nall, share), BF16),
             pltpu.VMEM((nall, B), jnp.int32),
             pltpu.VMEM((nall, 3 * B), BF16),
@@ -350,7 +386,7 @@
             pltpu.VMEM((SIDE, k // octet, k), F32),
             pltpu.VMEM((k, k), F32),
             dma((nr - 1, nch)), dma((nr - 1, nch)),
-            dma((nr - 1,)), dma((nr - 1,)), dma((2,)), dma((2,)), dma((4,)), dma((nch,)),
+            dma((nr - 1,)), dma((nr - 1,)), dma((2,)), dma((2,)), dma((4,)), dma((nch,)), dma((nch,)),
             dma((octet - 1,)), dma((octet - 1,)), dma((SIDE - 1,)), dma((SIDE - 1,)),
             dma((SIDE - 1,)), dma((SIDE - 1,)), dma((octet - 1,)), dma((octet - 1,)),
         ],
@@ -363,10 +399,10 @@
         functools.partial(factor_kernel, scale),
         grid=(share // tile,),
         out_shape=(jax.ShapeDtypeStruct((share, k), F32), jax.ShapeDtypeStruct((k, k), F32)),
-        in_specs=[pl.BlockSpec((tile, 2 * k), lambda i: (i, 0)), pl.BlockSpec((k, k), lambda i: (0, 0))],
+        in_specs=[hbm_spec, vmem_spec],
         out_specs=(pl.BlockSpec((tile, k), lambda i: (i, 0)), pl.BlockSpec((k, k), lambda i: (0, 0))),
-        scratch_shapes=[pltpu.VMEM((2 * k, 2 * k), BF16)],
-        compiler_params=pltpu.CompilerParams(dimension_semantics=("arbitrary",)),
+        scratch_shapes=[pltpu.VMEM((2 * k, 2 * k), BF16), pltpu.VMEM((share, 2 * k), BF16), dma],
+        compiler_params=pltpu.CompilerParams(dimension_semantics=("arbitrary",), vmem_limit_bytes=32 << 20),
     )(hl, gram)
     return q, u
 

time: 86.6 us -> 70.6 us (0.82)
  Pallas kernels: 82.5 us -> 65.1 us
  local copies, waits for them, and re-layouts: 3.04 us -> 4.61 us
    pallas_call x1, Pallas kernels: 24.7 us -> 9.06 us  [local(): pl.pallas_call(functools.partial(factor_kernel, scale), grid=(share // ti...]
    pallas_call x1, Pallas kernels: 57.9 us -> 56 us  [local(): pl.pallas_call(functools.partial(sketch_kernel, nr, ns), out_shape=(jax.S...]
    unnamed x4, local copies, waits for them, and re-layouts: 2.2 us -> 3.77 us
where the time goes in v3:
time: 70.6 us; the launch traced here: 70.3 us
  Pallas kernels  65.1 us (92%)
  local copies, waits for them, and re-layouts  4.61 us (7%)
    pallas_call x1, Pallas kernels, local(): pl.pallas_call(functools.partial(sketch_kernel, nr, ns), out_shape=(jax.S...  56 us
    pallas_call x1, Pallas kernels, local(): pl.pallas_call(functools.partial(factor_kernel, scale), grid=(share // ti...  9.06 us
    unnamed x4, local copies, waits for them, and re-layouts  3.77 us

profile of v3, /device:TPU:1, one launch (start us, length us, event | category | flops | bytes accessed | tf_op | source)
XLA Modules:
  0.0 70.3 jit_solution(13886946864482474362)
XLA Ops:
  0.6 0.8 %broadcast_in_dim.7 = s32[32]{0:T(128)S(1)} reshape(s32[4,8]{1,0:T(4,128)} %param.5) | data formatting | bytes 256 | tf_op jit(solution)/shard_map/broadcast_in_dim | solution.py:367
  1.4 0.1 broadcast_in_dim.8.o_hbm
  1.5 0.0 copy-start.1
  1.5 1.6 %copy-done.1 = bf16[4,8,32768]{2,1,0:T(8,128)(2,1)S(1)} copy-done((bf16[4,8,32768]{2,1,0:T(8,128)(2,1)S(1)}, bf16[4,8,32768]{2,1,0:T(8,128)(2,1)}, u32[]{:S(2)}) %copy-start.1) | copy-done | bytes 2097176
  3.1 56.0 %shard_map.50 = (bf16[8192,256]{1,0:T(8,128)(2,1)}, f32[128,128]{1,0:T(8,128)S(1)}) custom-call(bf16[32,32768]{1,0:T(8,128)(2,1)S(1)} %bitcast.1, s32[32,128]{1,0:T(8,128)S(1)} %broadcast_in_dim.8.o_hbm, bf16[32768,128]{1,0:T(8,128)(2,1)} %p_hbm.1), custom_call_target="tpu_custom_call" | custom-call | tf_op jit(solution)/shard_map/pallas_call | solution.py:371
  59.1 0.0 copy-start
  59.1 2.2 %copy-done = bf16[8192,256]{1,0:T(8,128)(2,1)S(1)} copy-done((bf16[8192,256]{1,0:T(8,128)(2,1)S(1)}, bf16[8192,256]{1,0:T(8,128)(2,1)}, u32[]{:S(2)}) %copy-start) | copy-done | bytes 4194328
  61.3 9.1 %shard_map.51 = (f32[8192,128]{1,0:T(8,128)}, f32[128,128]{1,0:T(8,128)}) custom-call(bf16[8192,256]{1,0:T(8,128)(2,1)S(1)} %copy-done, f32[128,128]{1,0:T(8,128)S(1)} %get-tuple-element.5.g_ref), custom_call_target="tpu_custom_call" | custom-call | tf_op jit(solution)/shard_map/pallas_call | solution.py:398
Async XLA Ops:
  1.5 1.6 %copy-start.1 = (bf16[4,8,32768]{2,1,0:T(8,128)(2,1)S(1)}, bf16[4,8,32768]{2,1,0:T(8,128)(2,1)}, u32[]{:S(2)}) copy-start(bf16[4,8,32768]{2,1,0:T(8,128)(2,1)} %param.4) | copy-start | bytes 6291460
  59.1 2.2 %copy-start = (bf16[8192,256]{1,0:T(8,128)(2,1)S(1)}, bf16[8192,256]{1,0:T(8,128)(2,1)}, u32[]{:S(2)}) copy-start(bf16[8192,256]{1,0:T(8,128)(2,1)} %get-tuple-element.4.hl_hbm) | copy-start | bytes 12582916

commit v4 on v3

--- a/solution.py
+++ b/solution.py
@@ -194,7 +194,8 @@
         band = pltpu.roll(diag, 0, 1, stride=1, stride_axis=0)
         bh, bl = split(band)
         piece = pbuf[pl.ds(p0, 3 * B), :]
-        sk = dot(bh, piece, ((1,), (0,))) + dot(bl, piece, ((1,), (0,)))
+        both = dot(jnp.concatenate([bh, bl], axis=0), piece, ((1,), (0,)))
+        sk = both[:B] + both[B:]
         hi, lo = split(sk)
         hl_ref[pl.ds(p0, B), 0:B] = hi
         hl_ref[pl.ds(p0, B), B:2 * B] = lo
@@ -363,7 +364,7 @@
     nall = nr * nloc
     nch = share // CHUNK
     octet = 2 * nr
-    coeffs = band_coeffs.reshape(nloc, rows)
+    coeffs = pltpu.with_memory_space_constraint(band_coeffs.reshape(nloc, rows), pltpu.HBM)
     offs = jnp.broadcast_to(band_offsets.reshape(nloc, 1), (nloc, B))
     hbm_spec = pl.BlockSpec(memory_space=pltpu.HBM)
     vmem_spec = pl.BlockSpec(memory_space=pltpu.VMEM)
@@ -392,7 +393,7 @@
         ],
         compiler_params=pltpu.CompilerParams(
             collective_id=0, has_side_effects=True, vmem_limit_bytes=48 << 20),
-    )(coeffs, offs, probes)
+    )(coeffs, offs, pltpu.with_memory_space_constraint(probes, pltpu.HBM))
     scale = math.sqrt(rows * ns)
     tile = 1024
     q, u = pl.pallas_call(

time: 70.6 us -> 68.1 us (0.965)
  local copies, waits for them, and re-layouts: 4.61 us -> 0.84 us
  Pallas kernels: 65.1 us -> 66.4 us
    unnamed x4 -> x0, local copies, waits for them, and re-layouts: 3.77 us -> none
    pallas_call x1, Pallas kernels: 56 us -> 57.3 us  [local(): pl.pallas_call(functools.partial(sketch_kernel, nr, ns), out_shape=(jax.S...]
where the time goes in v4:
time: 68.1 us; the launch traced here: 67.9 us
  Pallas kernels  66.4 us (98%)
  local copies, waits for them, and re-layouts  0.84 us (1%)
    pallas_call x1, Pallas kernels, local(): pl.pallas_call(functools.partial(sketch_kernel, nr, ns), out_shape=(jax.S...  57.3 us
    pallas_call x1, Pallas kernels, local(): pl.pallas_call(functools.partial(factor_kernel, scale), grid=(share // ti...  9.09 us

profile of v4, /device:TPU:1, one launch (start us, length us, event | category | flops | bytes accessed | tf_op | source)
XLA Modules:
  0.0 67.9 jit_solution(17311485469411771981)
XLA Ops:
  0.6 0.8 %broadcast_in_dim.7 = s32[32]{0:T(128)S(1)} reshape(s32[4,8]{1,0:T(4,128)} %param.5) | data formatting | bytes 256 | tf_op jit(solution)/shard_map/broadcast_in_dim | solution.py:368
  1.4 0.1 broadcast_in_dim.8.o_hbm
  1.5 57.3 %shard_map.50 = (bf16[8192,256]{1,0:T(8,128)(2,1)S(1)}, f32[128,128]{1,0:T(8,128)S(1)}) custom-call(bf16[32,32768]{1,0:T(8,128)(2,1)} %bitcast.1, s32[32,128]{1,0:T(8,128)S(1)} %broadcast_in_dim.8.o_hbm, bf16[32768,128]{1,0:T(8,128)(2,1)} %p_hbm.1), custom_call_target="tpu_custom_call" | custom-call | tf_op jit(solution)/shard_map/pallas_call | solution.py:372
  58.8 9.1 %shard_map.51 = (f32[8192,128]{1,0:T(8,128)}, f32[128,128]{1,0:T(8,128)}) custom-call(bf16[8192,256]{1,0:T(8,128)(2,1)S(1)} %get-tuple-element.4.hl_hbm, f32[128,128]{1,0:T(8,128)S(1)} %get-tuple-element.5.g_ref), custom_call_target="tpu_custom_call" | custom-call | tf_op jit(solution)/shard_map/pallas_call | solution.py:399

commit v5 on v4

--- a/solution.py
+++ b/solution.py
@@ -188,23 +188,20 @@
     main.wait()
     g_ref[...] = jnp.zeros_like(g_ref)
 
-    def block(p0):
-        cols = cbuf[:, pl.ds(p0, B)]
-        diag = dot(cols, sel[...], ((0,), (0,)))
-        band = pltpu.roll(diag, 0, 1, stride=1, stride_axis=0)
-        bh, bl = split(band)
-        piece = pbuf[pl.ds(p0, 3 * B), :]
-        both = dot(jnp.concatenate([bh, bl], axis=0), piece, ((1,), (0,)))
-        sk = both[:B] + both[B:]
-        hi, lo = split(sk)
-        hl_ref[pl.ds(p0, B), 0:B] = hi
-        hl_ref[pl.ds(p0, B), B:2 * B] = lo
-
     def step(i, _):
         base = pl.multiple_of(i * (UNROLL * B), UNROLL * B)
+        cols = cbuf[:, pl.ds(base, UNROLL * B)]
+        diag = dot(cols, sel[...], ((0,), (0,)))
+        bands = [pltpu.roll(diag[u * B:(u + 1) * B], 0, 1, stride=1, stride_axis=0) for u in range(UNROLL)]
+        rows_of = []
         for u in range(UNROLL):
-            block(base + u * B)
-        hl = hl_ref[pl.ds(base, UNROLL * B), :]
+            bh, bl = split(bands[u])
+            piece = pbuf[pl.ds(base + u * B, 3 * B), :]
+            both = dot(jnp.concatenate([bh, bl], axis=0), piece, ((1,), (0,)))
+            rows_of.append(both[:B] + both[B:])
+        hi, lo = split(jnp.concatenate(rows_of, axis=0))
+        hl = jnp.concatenate([hi, lo], axis=1)
+        hl_ref[pl.ds(base, UNROLL * B), :] = hl
         g_ref[...] += dot(hl, hl, ((0,), (0,)))
         return 0
 

time: 68.1 us -> 62.1 us (0.912)
  Pallas kernels: 66.4 us -> 60.4 us
    pallas_call x1, Pallas kernels: 57.3 us -> 51.3 us  [local(): pl.pallas_call(functools.partial(sketch_kernel, nr, ns), out_shape=(jax.S...]
where the time goes in v5:
time: 62.1 us; the launch traced here: 61.9 us
  Pallas kernels  60.4 us (97%)
  local copies, waits for them, and re-layouts  0.84 us (1%)
  between operations  0.64 us (1%)
    pallas_call x1, Pallas kernels, local(): pl.pallas_call(functools.partial(sketch_kernel, nr, ns), out_shape=(jax.S...  51.3 us
    pallas_call x1, Pallas kernels, local(): pl.pallas_call(functools.partial(factor_kernel, scale), grid=(share // ti...  9.08 us

profile of v5, /device:TPU:1, one launch (start us, length us, event | category | flops | bytes accessed | tf_op | source)
XLA Modules:
  0.0 61.9 jit_solution(13695442694729582717)
XLA Ops:
  0.6 0.8 %broadcast_in_dim.7 = s32[32]{0:T(128)S(1)} reshape(s32[4,8]{1,0:T(4,128)} %param.5) | data formatting | bytes 256 | tf_op jit(solution)/shard_map/broadcast_in_dim | solution.py:365
  1.4 0.1 broadcast_in_dim.8.o_hbm
  1.5 51.3 %shard_map.50 = (bf16[8192,256]{1,0:T(8,128)(2,1)S(1)}, f32[128,128]{1,0:T(8,128)S(1)}) custom-call(bf16[32,32768]{1,0:T(8,128)(2,1)} %bitcast.1, s32[32,128]{1,0:T(8,128)S(1)} %broadcast_in_dim.8.o_hbm, bf16[32768,128]{1,0:T(8,128)(2,1)} %p_hbm.1), custom_call_target="tpu_custom_call" | custom-call | tf_op jit(solution)/shard_map/pallas_call | solution.py:369
  52.8 9.1 %shard_map.51 = (f32[8192,128]{1,0:T(8,128)}, f32[128,128]{1,0:T(8,128)}) custom-call(bf16[8192,256]{1,0:T(8,128)(2,1)S(1)} %get-tuple-element.4.hl_hbm, f32[128,128]{1,0:T(8,128)S(1)} %get-tuple-element.5.g_ref), custom_call_target="tpu_custom_call" | custom-call | tf_op jit(solution)/shard_map/pallas_call | solution.py:396
